TPU v7x, 32 devices: a whole 2x2x4 slice. The times are simulated.
32 devices in a mesh: group: 8 (over y, x, core), ep: 4 (over z).
Axes of the slice: x: 2, y: 2, z: 4, core: 2. Of those that a mesh axis runs over, the one named last changes fastest.
Arguments:
- tokens: bfloat16 [1024, 3584], P(('group', 'ep')), may hold values from -6 to 6
- expert_ids: int32 [1024, 8], P(('group', 'ep')), may hold values from 0 to 31, as said below
- gate_scores: float32 [1024, 8], P(('group', 'ep')), may hold values from 0.05 to 0.35
- replica_pick: int32 [1024, 8], P(('group', 'ep')), may hold values from 0 to 8
- replica_hot: int32 [4], replicated, may hold values from 0 to 7
- gate_weight: bfloat16 [32, 3584, 1024], P(('group', 'ep')), may hold values from -0.09375 to 0.09375
- up_weight: bfloat16 [32, 3584, 1024], P(('group', 'ep')), may hold values from -0.09375 to 0.09375
- down_weight: bfloat16 [32, 1024, 3584], P(('group', 'ep')), may hold values from -0.1875 to 0.1875
Outputs:
- mixed: bfloat16 [1024, 3584], P(('group', 'ep'))
- slot_load: float32 [32, 2], P(('group', 'ep'))
Inputs may be any that keep to these rules, and one draw needn't show every extreme that they name: `expert_ids`: each row names 8 different experts; in each aligned block of 16 rows (one micro-batch of one device) no expert is named by more than 5 rows, and the expert replica_hot[c] * 4 + c of each ep index c is named by exactly 5 rows.
All inputs are finite; a program needn't handle non-finite values.
Results may differ from a plain program's by a relative error of at most 0.0057.
Values may be sent and summed in bfloat16 or wider, within the bound.
A program may use at most 128 MiB of HBM per device.

v0:
```python
import jax
import jax.numpy as jnp
from jax import lax
from jax.sharding import PartitionSpec as P

AXES = ("group", "ep")


def body(
    tokens, expert_ids, gate_scores, replica_pick, replica_hot, gate_weight, up_weight, down_weight
):
    ngroup = lax.axis_size("group")
    ep_count = lax.axis_size("ep")
    device_count = ngroup * ep_count
    group_index = lax.axis_index("group")
    ep_index = lax.axis_index("ep")
    me = group_index * ep_count + ep_index
    tok_dev, width = tokens.shape
    top_count = expert_ids.shape[1]
    micro_len = tok_dev // 2
    most = (micro_len * top_count + device_count - 1) // device_count + 1
    capacity = 2 * most * device_count
    routing = jnp.concatenate(
        [expert_ids.astype(jnp.float32), replica_pick.astype(jnp.float32), gate_scores], axis=1
    )
    routing = lax.all_gather(routing, AXES, axis=0, tiled=True)
    every = lax.all_gather(tokens, AXES, axis=0, tiled=True)
    ids = routing[:, :top_count].astype(jnp.int32)
    picks = routing[:, top_count : 2 * top_count].astype(jnp.int32)
    gates = routing[:, 2 * top_count :]
    hot = replica_hot[ep_index]
    in_column = ids % ep_count == ep_index
    replicated = in_column & (ids // ep_count == hot) & (picks < ngroup)
    primary_load = jnp.sum(((ids == me) & ~replicated).astype(jnp.float32))
    replica_load = jnp.sum((replicated & (picks == group_index)).astype(jnp.float32))
    loads = jnp.stack([primary_load, replica_load])[None, :] / top_count
    chosen = ids == me
    mask = jnp.any(chosen, axis=1)
    scale = jnp.sum(jnp.where(chosen, gates, 0.0), axis=1)
    place = jnp.where(mask, jnp.cumsum(mask.astype(jnp.int32)) - 1, -1)
    spot = place[None, :] == jnp.arange(capacity, dtype=jnp.int32)[:, None]
    select = spot.astype(jnp.bfloat16)
    row_scale = jnp.sum(jnp.where(spot, scale[None, :], 0.0), axis=1)
    picked = jnp.dot(select, every, preferred_element_type=jnp.float32).astype(jnp.bfloat16)
    gate_act = jnp.dot(picked, gate_weight[0], preferred_element_type=jnp.float32)
    up_act = jnp.dot(picked, up_weight[0], preferred_element_type=jnp.float32)
    hidden = (jax.nn.silu(gate_act) * up_act).astype(jnp.bfloat16)
    pair_out = jnp.dot(hidden, down_weight[0], preferred_element_type=jnp.float32)
    scaled = (pair_out * row_scale[:, None]).astype(jnp.bfloat16)
    spread = jnp.dot(select.T, scaled, preferred_element_type=jnp.float32).astype(jnp.bfloat16)
    mixed = lax.psum_scatter(spread, AXES, scatter_dimension=0, tiled=True)
    return (mixed, loads)


def solution(mesh):
    rows = P(AXES, None)
    return jax.shard_map(
        body,
        mesh=mesh,
        in_specs=(
            rows,
            rows,
            rows,
            rows,
            P(),
            P(AXES, None, None),
            P(AXES, None, None),
            P(AXES, None, None),
        ),
        out_specs=(rows, rows),
        check_vma=False,
    )
```

profile of v0, /device:TPU:0, one launch (start us, length us, event | category | flops | bytes accessed | tf_op | source)
XLA Modules:
  0.0 289.5 jit_solution(16672365116198364456)
XLA Ops:
  7.2 0.0 all-gather.3.cloned.1.call-start
  7.2 0.7 all-gather.3.cloned.1.call-update
  7.9 0.0 reduce-scatter.2.cloned.1.call-start
  8.0 0.7 convert_element_type.39
  8.6 0.7 convert_element_type.38
  9.3 0.7 maximum_bitcast_fusion
  10.0 76.5 %all-gather = f32[32,32,24]{1,2,0:T(8,128)S(1)} all-gather(f32[1,32,24]{1,2,0:T(8,128)S(1)} %maximum_bitcast_fusion), channel_id=1, replica_groups=mesh['group'=8,'ep'=4] {'group','ep'}, dimensions={0}, use_global_device_ids=true | all-gather | bytes 101376 | tf_op jit(solution)/shard_map/all_gather | solution.py:26
  86.6 0.1 copy.12
  86.6 0.2 reshape.71
  86.8 1.2 dynamic_slice.3
  88.1 0.7 fusion.30
  88.8 0.3 reduce-window.9
  89.1 0.1 slice.17
  89.2 0.1 slice_reduce_fusion
  89.3 0.7 convert_reduce_fusion
  90.0 0.1 bitcast_select_fusion
  90.1 0.2 select_reduce_fusion
  90.3 0.0 all-gather.3.cloned.1.call-done
  90.3 5.6 %convolution_convert_fusion.1 = bf16[320,3584]{1,0:T(8,128)(2,1)S(1)} fusion(bf16[1024,3584]{1,0:T(8,128)(2,1)} %all-gather.3.cloned.1.call-done, s32[1024]{0:T(1024)S(1)} %bitcast_select_fusion), kind=kOutput, calls=%fused_computation.9 | convolution fusion | flops 2350284800 | bytes 9637888 | tf_op jit(solution)/shard_map/dot_general | solution.py:44
  95.9 0.0 copy-start
  95.9 1.4 copy-done
  97.3 6.7 %fusion.4 = f32[320,1024]{1,0:T(8,128)} fusion(bf16[320,3584]{1,0:T(8,128)(2,1)S(1)} %convolution_convert_fusion.1, bf16[1,3584,1024]{2,1,0:T(8,128)(2,1)} %param.13), kind=kOutput, calls=%fused_computation.5 | convolution fusion | flops 2348810240 | bytes 10944512 | tf_op jit(solution)/shard_map/dot_general | solution.py:45
  104.0 11.2 %fusion.9 = bf16[320,3584]{1,0:T(8,128)(2,1)S(1)} fusion(bf16[1,1024,3584]{2,1,0:T(8,128)(2,1)} %param.15, f32[320]{0:T(512)S(1)} %select_reduce_fusion, bf16[320,3584]{1,0:T(8,128)(2,1)} %copy-done, bf16[1,3584,1024]{2,1,0:T(8,128)(2,1)} %param.14, f32[320,1024]{1,0:T(8,128)} %fusion.4), kind=kOutput, calls=%fused_computation.8 | convolution fusion | flops 4701880320 | bytes 20579584 | tf_op jit(solution)/shard_map/dot_general | solution.py:48
  115.2 6.1 %convolution_convert_fusion = bf16[1024,3584]{1,0:T(8,128)(2,1)} fusion(bf16[320,3584]{1,0:T(8,128)(2,1)S(1)} %fusion.9, s32[1024]{0:T(1024)S(1)} %bitcast_select_fusion), kind=kOutput, calls=%fused_computation | convolution fusion | flops 2352807936 | bytes 9637888 | tf_op jit(solution)/shard_map/dot_general | solution.py:50
  121.3 0.0 reduce-scatter.2.cloned.1.call-update
  121.3 1.8 maximum_multiply_fusion
  123.1 159.5 %reduce-scatter.2.cloned.1.call-done = bf16[32,3584]{1,0:T(8,128)(2,1)} async-done(((bf16[1024,3584]{1,0:T(8,128)(2,1)}), bf16[32,3584]{1,0:T(8,128)(2,1)}) %reduce-scatter.2.cloned.1.call-update) | async-done | bytes 229392 | tf_op jit(solution)/shard_map/reduce_scatter | solution.py:51
  (2 shorter events, 0.0 us)
Async XLA Ops:
  7.2 83.1 %all-gather.3.cloned.1.call-start = ((), (), s32[]{:S(2)}) async-start(), calls=%async_computation.1 | async-start | bytes 7569408 | tf_op jit(solution)/shard_map/all_gather | solution.py:27
  7.9 274.7 %reduce-scatter.2.cloned.1.call-start = ((), (), s32[]{:S(2)}) async-start(), calls=%async_computation.2 | async-start | bytes 7569408 | tf_op jit(solution)/shard_map/reduce_scatter | solution.py:51
  95.9 1.4 copy-start
Sparse Core Ops, SparseCore 0:
  10.8 77.1 all-gather.2
  121.4 161.1 reduce-scatter.1
where the time goes:
time: 290 us; the launch traced here: 289 us
  waiting for transfers between devices  160 us (55%)
  blocking collectives  76.5 us (26%)
  matrix products  29.6 us (10%)
  between operations  14.1 us (5%)
  other arithmetic  5.94 us (2%)
  local copies, waits for them, and re-layouts  3.07 us (1%)
    reduce_scatter x1, waiting for transfers between devices, body(): mixed = lax.psum_scatter(spread, AXES, scatter_dimension=0, tiled=True)  159 us
    all_gather x1, blocking collectives, body(): routing = lax.all_gather(routing, AXES, axis=0, tiled=True)  76.5 us
    dot_general x1, matrix products, body(): jnp.dot(hidden, down_weight[0], preferred_element_type=jnp.float32)  11.2 us
    dot_general x1, matrix products, body(): jnp.dot(picked, gate_weight[0], preferred_element_type=jnp.float32)  6.68 us
    dot_general x1, matrix products, body(): jnp.dot(select.T, scaled, preferred_element_type=jnp.float32)  6.09 us
  transfers between devices with their start and end apart: 2, of which 1 were waited for; matrix products, arithmetic and copies ran while one was open for 3% of the time, Pallas kernels for 0%

commit v1 on v0

--- a/solution.py
+++ b/solution.py
@@ -23,8 +23,11 @@
     routing = jnp.concatenate(
         [expert_ids.astype(jnp.float32), replica_pick.astype(jnp.float32), gate_scores], axis=1
     )
-    routing = lax.all_gather(routing, AXES, axis=0, tiled=True)
-    every = lax.all_gather(tokens, AXES, axis=0, tiled=True)
+    routing, every = jnp.split(
+        lax.all_gather(jnp.concatenate([routing, tokens], axis=1), AXES, axis=0, tiled=True),
+        [routing.shape[1]],
+        axis=1,
+    )
     ids = routing[:, :top_count].astype(jnp.int32)
     picks = routing[:, top_count : 2 * top_count].astype(jnp.int32)
     gates = routing[:, 2 * top_count :]

time: 290 us -> 329 us (1.13)
  waiting for transfers between devices: 160 us -> 269 us
  blocking collectives: 76.5 us -> 0 us
  other arithmetic: 5.94 us -> 9.34 us
    all_gather x1, waiting for transfers between devices: 0.01 us -> 109 us  [body(): lax.all_gather(jnp.concatenate([routing, tokens], axis=1), AXES, axis=0,...]
    all_gather x1 -> x0, blocking collectives: 76.5 us -> none  [body(): routing = lax.all_gather(routing, AXES, axis=0, tiled=True)]
  transfers between devices with their start and end apart: 2 -> 2, of which waited for: 1 -> 2; matrix products, arithmetic and copies ran while one was open for 3% -> 1% of each run, Pallas kernels for 0% -> 0%
where the time goes in v1:
time: 329 us
  waiting for transfers between devices  269 us (82%)
  matrix products  31.9 us (10%)
  between operations  14.1 us (4%)
  other arithmetic  9.34 us (3%)
  local copies, waits for them, and re-layouts  4.28 us (1%)
    reduce_scatter x1, waiting for transfers between devices, body(): mixed = lax.psum_scatter(spread, AXES, scatter_dimension=0, tiled=True)  161 us
    all_gather x1, waiting for transfers between devices, body(): lax.all_gather(jnp.concatenate([routing, tokens], axis=1), AXES, axis=0,...  109 us
    dot_general x1, matrix products, body(): jnp.dot(hidden, down_weight[0], preferred_element_type=jnp.float32)  12.2 us
    dot_general x1, matrix products, body(): jnp.dot(select, every, preferred_element_type=jnp.float32)  8.27 us
    dot_general x1, matrix products, body(): jnp.dot(select.T, scaled, preferred_element_type=jnp.float32)  7.72 us
  transfers between devices with their start and end apart: 2, of which 2 were waited for; matrix products, arithmetic and copies ran while one was open for 1% of the time, Pallas kernels for 0%

profile of v1, /device:TPU:0, one launch (start us, length us, event | category | flops | bytes accessed | tf_op | source)
XLA Modules:
  0.0 329.0 jit_solution(13943967341426092146)
XLA Ops:
  7.2 0.0 all-gather.2.cloned.1.call-start
  7.2 0.7 convert_element_type.41
  7.9 0.1 copy.16
  8.0 0.7 convert_element_type.42
  8.7 0.1 copy.17
  8.7 0.8 copy.18
  9.5 1.9 concatenate.10
  11.4 0.0 all-gather.2.cloned.1.call-update
  11.5 0.0 reduce-scatter.2.cloned.1.call-start
  11.5 1.2 dynamic_slice.3
  12.8 108.6 %all-gather.2.cloned.1.call-done = f32[1024,3608]{1,0:T(8,128)} async-done(((f32[32,3608]{1,0:T(8,128)}), f32[1024,3608]{1,0:T(8,128)}) %all-gather.2.cloned.1.call-update) | async-done | bytes 14778384 | tf_op jit(solution)/shard_map/all_gather | solution.py:27
  121.4 2.8 fusion.35
  124.2 0.3 reduce-window.9
  124.5 0.1 slice.20
  124.6 0.1 slice_reduce_fusion
  124.7 0.1 bitcast_select_fusion
  124.8 0.0 slice-start
  124.8 2.6 convert_reduce_fusion
  127.4 0.2 select_reduce_fusion
  127.7 0.0 slice-start.1
  127.7 8.3 %fusion.14 = bf16[320,3584]{1,0:T(8,128)(2,1)S(1)} fusion(f32[1024,3608]{1,0:T(8,128)} %all-gather.2.cloned.1.call-done, s32[1024]{0:T(1024)S(1)} %bitcast_select_fusion), kind=kOutput, calls=%fused_computation.11 | convolution fusion | flops 2349137920 | bytes 9637888 | tf_op jit(solution)/shard_map/dot_general | solution.py:47
  135.9 0.0 slice-done
  136.0 0.0 slice-done.1
  136.0 3.7 %fusion.6 = f32[320,1024]{1,0:T(8,128)} fusion(bf16[320,3584]{1,0:T(8,128)(2,1)S(1)} %fusion.14, bf16[1,3584,1024]{2,1,0:T(8,128)(2,1)S(1)} %bitcast.30), kind=kOutput, calls=%fused_computation.7 | convolution fusion | flops 2348810240 | bytes 10944512 | tf_op jit(solution)/shard_map/dot_general | solution.py:48
  139.7 12.2 %fusion.11 = bf16[320,3584]{1,0:T(8,128)(2,1)} fusion(bf16[1,1024,3584]{2,1,0:T(8,128)(2,1)} %param.15, f32[320]{0:T(512)S(1)} %select_reduce_fusion, bf16[320,3584]{1,0:T(8,128)(2,1)S(1)} %fusion.14, bf16[1,3584,1024]{2,1,0:T(8,128)(2,1)} %param.14, f32[320,1024]{1,0:T(8,128)} %fusion.6), kind=kOutput, calls=%fused_computation.10 | convolution fusion | flops 4701880320 | bytes 20579584 | tf_op jit(solution)/shard_map/dot_general | solution.py:51
  151.9 7.7 %convolution_convert_fusion = bf16[1024,3584]{1,0:T(8,128)(2,1)} fusion(bf16[320,3584]{1,0:T(8,128)(2,1)} %fusion.11, s32[1024]{0:T(1024)S(1)} %bitcast_select_fusion), kind=kOutput, calls=%fused_computation.2 | convolution fusion | flops 2352807936 | bytes 9637888 | tf_op jit(solution)/shard_map/dot_general | solution.py:53
  159.6 0.0 reduce-scatter.2.cloned.1.call-update
  159.6 1.9 maximum_multiply_fusion
  161.5 160.6 %reduce-scatter.2.cloned.1.call-done = bf16[32,3584]{1,0:T(8,128)(2,1)} async-done(((bf16[1024,3584]{1,0:T(8,128)(2,1)}), bf16[32,3584]{1,0:T(8,128)(2,1)}) %reduce-scatter.2.cloned.1.call-update) | async-done | bytes 229392 | tf_op jit(solution)/shard_map/reduce_scatter | solution.py:54
  (3 shorter events, 0.0 us)
Async XLA Ops:
  7.2 114.2 %all-gather.2.cloned.1.call-start = ((), (), s32[]{:S(2)}) async-start(), calls=%async_computation.1 | async-start | bytes 15679488 | tf_op jit(solution)/shard_map/all_gather | solution.py:27
  11.5 310.7 %reduce-scatter.2.cloned.1.call-start = ((), (), s32[]{:S(2)}) async-start(), calls=%async_computation.2 | async-start | bytes 7569408 | tf_op jit(solution)/shard_map/reduce_scatter | solution.py:54
  124.8 11.1 %slice-start = ((s8[7340032]{0:T(1024)(128)(4,1)}), s8[4194304]{0:T(1024)(128)(4,1)S(1)}, s32[]{:S(2)}) async-start(s8[7340032]{0:T(1024)(128)(4,1)} %bitcast.29), calls=%async_computation.3 | async-start | bytes 8388608
  127.7 8.3 %slice-start.1 = ((s8[7340032]{0:T(1024)(128)(4,1)}), s8[3145728]{0:T(1024)(128)(4,1)S(1)}, s32[]{:S(2)}) async-start(s8[7340032]{0:T(1024)(128)(4,1)} %bitcast.29), calls=%async_computation.4 | async-start | bytes 6291456
Sparse Core Ops, SparseCore 0:
  11.6 109.7 all-gather.1
  159.8 162.3 reduce-scatter.1
